TPU v7x, 32 devices: a whole 2x2x4 slice. The times are simulated.
32 devices in a mesh: gx: 8 (over z, x), gy: 4 (over y, core).
Axes of the slice: x: 2, y: 2, z: 4, core: 2. Of those that a mesh axis runs over, the one named last changes fastest.
Arguments:
- probe_seeds: int32 [4], replicated, may hold values from 0 to 1048575
- damping: float32 [512, 1024], P('gx', 'gy'), may hold values from 0.2 to 1
- coupling_x: float32 [512, 1024], P('gx', 'gy'), may hold values from 0.05 to 0.5
- coupling_y: float32 [512, 1024], P('gx', 'gy'), may hold values from 0.05 to 0.5
- sensor_count: int32 [8, 4], P('gx', 'gy'), may hold values from 1 to 256, as said below
- sensor_cells: int32 [8, 4, 256], P('gx', 'gy'), may hold values from 0 to 16383
- obs_weight: float32 [8, 4, 256, 256], P('gx', 'gy'), as said below
Outputs:
- solution: float32 [4, 512, 1024], P(None, 'gx', 'gy')
- trace_estimate: float32 [], replicated
Inputs may be any that keep to these rules, and one draw needn't show every extreme that they name: `sensor_count`: at most 256, and some block has exactly 256 in every draw; blocks near a few cluster centres are far busier than the rest. `sensor_cells`: cells within the block, numbered row by row. `obs_weight`: each block's matrix is symmetric positive definite.
All inputs are finite; a program needn't handle non-finite values.
Results may differ from a plain program's by a relative error of at most 0.0003.
Values sent between devices are 32-bit elements; how exact they have to be, the bound alone decides.
No kernel may reach another device: no remote copies, remote signals or barrier semaphores. Data moves between devices by JAX's collectives and lax.ppermute only.
A program may use at most 64 MiB of HBM per device.

v0:
```python
import jax
import jax.numpy as jnp
from jax import lax
from jax.sharding import PartitionSpec as P


def with_halo(cells, sides, width):
    for axis, dim in sides:
        count = lax.axis_size(axis)
        head = lax.slice_in_dim(cells, 0, width, axis=dim)
        tail = lax.slice_in_dim(cells, cells.shape[dim] - width, cells.shape[dim], axis=dim)
        cells = jnp.concatenate(
            [
                lax.ppermute(tail, axis, [(i, (i + 1) % count) for i in range(count)]),
                cells,
                lax.ppermute(head, axis, [((i + 1) % count, i) for i in range(count)]),
            ],
            axis=dim,
        )
    return cells


def shifted(value, axis, steps):
    count = lax.axis_size(axis)
    pairs = [(source, (source + steps) % count) for source in range(count)]
    return lax.ppermute(value, axis, pairs)


def rademacher(seeds, row_ids, col_ids):
    mixed = (
        seeds[:, None, None] * 668265261
        + row_ids[None, :, None] * 374761393
        + col_ids[None, None, :] * 1103515245
    )
    mixed = (mixed ^ mixed >> 16 & 65535) * 73244475
    mixed = (mixed ^ mixed >> 16 & 65535) * 73244475
    mixed = mixed ^ mixed >> 16 & 65535
    bit_value = mixed >> 7 & 1
    return (2 * bit_value - 1).astype(jnp.float32)


def apply_region(padded, damping, face_rows, face_cols):
    centre = padded[:, 1:-1, 1:-1]
    return (
        damping * centre
        + face_rows[1:] * (centre - padded[:, 2:, 1:-1])
        + face_rows[:-1] * (centre - padded[:, :-2, 1:-1])
        + face_cols[:, 1:] * (centre - padded[:, 1:-1, 2:])
        + face_cols[:, :-1] * (centre - padded[:, 1:-1, :-2])
    )


def rim_one(field):
    return with_halo(field, (("gx", 1), ("gy", 2)), 1)


def curvature(first, second):
    return lax.psum(jnp.sum(first * second, axis=(1, 2)), ("gx", "gy"))


def per_device(
    probe_seeds, damping, coupling_x, coupling_y, sensor_count, sensor_cells, obs_weight
):
    block_rows, block_cols = damping.shape
    row_ids = lax.axis_index("gx") * block_rows + jnp.arange(block_rows, dtype=jnp.int32)
    col_ids = lax.axis_index("gy") * block_cols + jnp.arange(block_cols, dtype=jnp.int32)
    probes = rademacher(probe_seeds, row_ids, col_ids)
    before_rows = shifted(coupling_x[-1:, :], "gx", 1)
    before_cols = shifted(coupling_y[:, -1:], "gy", 1)
    inner = (
        damping,
        jnp.concatenate([before_rows, coupling_x], 0),
        jnp.concatenate([before_cols, coupling_y], 1),
    )
    count = sensor_count[0, 0]
    cell_ids = sensor_cells[0, 0]
    weight = obs_weight[0, 0]
    mask = (jnp.arange(weight.shape[0]) < count).astype(jnp.float32)

    def observe(field):
        flat = field.reshape(field.shape[0], -1)
        sampled = jnp.take(flat, cell_ids, axis=1) * mask
        weighted = jnp.dot(sampled, weight, precision=lax.Precision.HIGHEST)
        weighted = weighted * mask
        return jnp.zeros_like(flat).at[:, cell_ids].add(weighted).reshape(field.shape)

    def operator_twice(field):
        once = apply_region(rim_one(field), *inner)
        return apply_region(rim_one(once), *inner)

    def hessian(field):
        return operator_twice(field) + observe(field)

    cells_total = block_rows * block_cols * lax.axis_size("gx") * lax.axis_size("gy")
    norm_start = jnp.full((probes.shape[0],), float(cells_total), jnp.float32)
    image = hessian(probes)
    first_step = norm_start / curvature(probes, image)
    solution = first_step[:, None, None] * probes
    residual = probes - first_step[:, None, None] * image
    residual_image = hessian(residual)
    norm_next, product = lax.psum(
        (
            jnp.sum(residual * residual, axis=(1, 2)),
            jnp.sum(residual * residual_image, axis=(1, 2)),
        ),
        ("gx", "gy"),
    )
    ratio = norm_next / norm_start
    direction = residual + ratio[:, None, None] * probes
    second_step = norm_next / (product - ratio * norm_next / first_step)
    solution = solution + second_step[:, None, None] * direction
    total = lax.psum(jnp.sum(probes * solution), ("gx", "gy"))
    return (solution, total / probes.shape[0])


def solution(mesh):
    placed = (
        P(),
        P("gx", "gy"),
        P("gx", "gy"),
        P("gx", "gy"),
        P("gx", "gy"),
        P("gx", "gy", None),
        P("gx", "gy", None, None),
    )
    return jax.shard_map(
        per_device,
        mesh=mesh,
        in_specs=placed,
        out_specs=(P(None, "gx", "gy"), P()),
        check_vma=False,
    )
```

profile of v0, /device:TPU:0, one launch (start us, length us, event | category | flops | bytes accessed | tf_op | source)
XLA Modules:
  0.0 211.1 jit_solution(12646196828088814270)
XLA Ops:
  0.6 0.0 copy-start
  0.6 0.0 copy-start.1
  0.7 0.0 copy-start.2
  0.7 0.0 copy-start.4
  0.7 0.7 broadcast_multiply_fusion.1
  1.5 0.1 broadcast_add_fusion
  1.5 0.2 add_convert_fusion.1
  1.8 6.1 %collective-permute-start = (f32[4,1,256]{2,1,0:T(1,128)S(1)}, f32[4,1,256]{2,1,0:T(1,128)S(1)}, u32[]{:S(2)}, u32[]{:S(2)}) collective-permute-start(f32[4,1,256]{2,1,0:T(1,128)S(1)} %get-tuple-element.26), channel_id=1, source_target_pairs={{4,0},{8,4},{12,8},{16,12},{20,16},{24,20},{28,24},{0,28},{5,1},{9... | collective-permute-start | bytes 12296 | tf_op jit(solution)/shard_map/ppermute | solution.py:16
  7.8 0.0 collective-permute-start.2
  7.8 0.8 slice.138
  8.6 0.0 collective-permute-start.4
  8.6 0.7 slice.132
  9.4 0.2 copy.33
  9.6 0.7 compare_select_fusion.1
  10.9 0.7 compare_and_fusion
  11.6 0.2 add_convert_fusion
  11.9 5.1 %copy.25 = f32[4,16384]{0,1:T(8,128)} copy(f32[4,16384]{1,0:T(4,128)S(1)} %add_convert_fusion) | data formatting | bytes 524288 | tf_op jit(solution)/shard_map/convert_element_type | solution.py:39
  16.9 4.1 %gather_fusion = f32[256,4]{1,0:T(8,128)S(1)} fusion(f32[4,16384]{0,1:T(8,128)} %copy.25, s32[1024]{0:T(1024)S(1)} %pad_clamp_fusion), kind=kCustom, calls=%fused_computation.clone | custom fusion | bytes 9216 | tf_op jit(solution)/shard_map/jit(_take)/gather | solution.py:82
  21.0 0.1 copy.26
  21.1 0.1 pad_maximum_fusion.36
  21.3 0.1 fusion.80
  21.4 1.7 collective-permute-start.5
  23.1 0.2 collective-permute-start.3
  23.2 2.7 %collective-permute-done.5 = f32[4,66,1]{2,1,0:T(8,128)S(1)} collective-permute-done((f32[4,66,1]{2,1,0:T(8,128)S(1)}, f32[4,66,1]{2,1,0:T(8,128)S(1)}, u32[]{:S(2)}, u32[]{:S(2)}) %collective-permute-start.5) | collective-permute-done | bytes 1088 | tf_op jit(solution)/shard_map/ppermute | solution.py:14
  26.0 0.6 collective-permute-done.3
  26.6 0.3 fusion.54
  26.9 4.8 %collective-permute-start.6 = (f32[4,1,256]{2,1,0:T(1,128)S(1)}, f32[4,1,256]{2,1,0:T(1,128)S(1)}, u32[]{:S(2)}, u32[]{:S(2)}) collective-permute-start(f32[4,1,256]{2,1,0:T(1,128)S(1)} %get-tuple-element.24), channel_id=1, source_target_pairs={{4,0},{8,4},{12,8},{16,12},{20,16},{24,20},{28,24},{0,28},{5,1},{9... | collective-permute-start | bytes 12296 | tf_op jit(solution)/shard_map/ppermute | solution.py:16
  31.7 0.2 fusion.5
  31.9 1.1 collective-permute-done.6
  33.0 5.0 %collective-permute-done.7 = f32[4,1,256]{2,1,0:T(1,128)S(1)} collective-permute-done((f32[4,1,256]{2,1,0:T(1,128)S(1)}, f32[4,1,256]{2,1,0:T(1,128)S(1)}, u32[]{:S(2)}, u32[]{:S(2)}) %collective-permute-start.7) | collective-permute-done | bytes 4128 | tf_op jit(solution)/shard_map/ppermute | solution.py:14
  38.0 0.1 fusion.79
  38.1 0.1 collective-permute-start.9
  38.2 1.7 collective-permute-start.8
  39.9 0.1 copy.27
  40.1 5.1 %scatter_custom_fusion = f32[4,16384]{0,1:T(8,128)} fusion(s32[256]{0:T(256)S(1)} %bitcast.37, f32[256,4]{1,0:T(8,128)S(1)} %copy.27, f32[]{:T(128)} %constant.53.clone.1), kind=kCustom, calls=%fused_computation.6 | custom fusion | flops 1024 | bytes 262148 | tf_op jit(solution)/shard_map/scatter-add | solution.py:85
  45.2 5.2 %copy.28 = f32[4,64,256]{2,1,0:T(8,128)S(1)} copy(f32[4,64,256]{0,2,1:T(8,128)} %bitcast.31) | data formatting | bytes 524288 | tf_op jit(solution)/shard_map/reshape | solution.py:85
  50.5 0.5 multiply_reduce_fusion.2
  51.0 36.9 %psum.28 = f32[4]{0:T(128)S(1)} all-reduce(f32[4]{0:T(128)S(1)} %get-tuple-element.9), channel_id=1, replica_groups=mesh['gx'=8,'gy'=4] {'gx','gy'}, use_global_device_ids=true, to_apply=%region_2.4 | all-reduce | flops 4 | bytes 32 | tf_op jit(solution)/shard_map/psum | solution.py:58
  87.9 0.3 multiply_reduce_fusion.1
  88.2 4.0 %collective-permute-start.10 = (f32[4,1,256]{2,1,0:T(1,128)S(1)}, f32[4,1,256]{2,1,0:T(1,128)S(1)}, u32[]{:S(2)}, u32[]{:S(2)}) collective-permute-start(f32[4,1,256]{2,1,0:T(1,128)S(1)} %get-tuple-element.22), channel_id=1, source_target_pairs={{4,0},{8,4},{12,8},{16,12},{20,16},{24,20},{28,24},{0,28},{5,1},{9... | collective-permute-start | bytes 12296 | tf_op jit(solution)/shard_map/ppermute | solution.py:16
  92.2 1.3 collective-permute-done.10
  93.6 5.0 %collective-permute-done.11 = f32[4,1,256]{2,1,0:T(1,128)S(1)} collective-permute-done((f32[4,1,256]{2,1,0:T(1,128)S(1)}, f32[4,1,256]{2,1,0:T(1,128)S(1)}, u32[]{:S(2)}, u32[]{:S(2)}) %collective-permute-start.11) | collective-permute-done | bytes 4128 | tf_op jit(solution)/shard_map/ppermute | solution.py:14
  98.6 0.1 fusion.78
  98.7 0.1 collective-permute-start.13
  98.7 1.7 collective-permute-start.12
  100.5 2.8 %collective-permute-done.13 = f32[4,66,1]{2,1,0:T(8,128)S(1)} collective-permute-done((f32[4,66,1]{2,1,0:T(8,128)S(1)}, f32[4,66,1]{2,1,0:T(8,128)S(1)}, u32[]{:S(2)}, u32[]{:S(2)}) %collective-permute-start.13) | collective-permute-done | bytes 1088 | tf_op jit(solution)/shard_map/ppermute | solution.py:14
  103.3 0.7 collective-permute-done.12
  104.0 0.3 fusion.29
  104.3 0.1 collective-permute-start.14
  104.3 2.0 collective-permute-start.15
  106.3 4.6 %copy.29 = f32[4,64,256]{0,2,1:T(8,128)} copy(f32[4,64,256]{2,1,0:T(8,128)S(1)} %get-tuple-element.8) | data formatting | bytes 524288 | tf_op jit(solution)/shard_map/sub | solution.py:99
  111.0 4.1 %gather_fusion.1 = f32[256,4]{1,0:T(8,128)S(1)} fusion(f32[4,16384]{0,1:T(8,128)} %bitcast.32, s32[1024]{0:T(1024)S(1)} %pad_clamp_fusion), kind=kCustom, calls=%fused_computation.1.clone | custom fusion | bytes 9216 | tf_op jit(solution)/shard_map/jit(_take)/gather | solution.py:82
  115.1 0.1 copy.30
  115.2 0.1 fusion.77
  115.3 0.5 collective-permute-start.17
  115.8 1.3 collective-permute-start.16
  117.1 0.2 fusion.4
  117.3 0.2 copy.31
  117.5 5.1 %scatter_custom_fusion.1 = f32[4,16384]{0,1:T(8,128)} fusion(s32[256]{0:T(256)S(1)} %bitcast.38, f32[256,4]{1,0:T(8,128)S(1)} %copy.31, f32[]{:T(128)} %constant.53.clone.1), kind=kCustom, calls=%fused_computation.4 | custom fusion | flops 1024 | bytes 262148 | tf_op jit(solution)/shard_map/scatter-add | solution.py:85
  122.6 5.2 %copy.32 = f32[4,64,256]{2,1,0:T(8,128)S(1)} copy(f32[4,64,256]{0,2,1:T(8,128)} %bitcast.30) | data formatting | bytes 524288 | tf_op jit(solution)/shard_map/reshape | solution.py:85
  127.9 0.4 fusion.17
  128.2 38.3 %all-reduce = (f32[4]{0:T(128)S(1)}, f32[4]{0:T(128)S(1)}) all-reduce(f32[4]{0:T(128)S(1)} %get-tuple-element.7, f32[4]{0:T(128)S(1)} %fusion.17), channel_id=1, replica_groups=mesh['gx'=8,'gy'=4] {'gx','gy'}, use_global_device_ids=true, to_apply=%region_4.6 | all-reduce | flops 8 | bytes 64 | tf_op jit(solution)/shard_map/psum | solution.py:101
  166.5 1.6 multiply_reduce_fusion
  168.1 41.2 %psum.31 = f32[]{:T(128)} all-reduce(f32[]{:T(128)} %get-tuple-element.5), channel_id=1, replica_groups=mesh['gx'=8,'gy'=4] {'gx','gy'}, use_global_device_ids=true, to_apply=%region_9.11 | all-reduce | flops 1 | bytes 8 | tf_op jit(solution)/shard_map/psum | solution.py:112
  (36 shorter events, 0.3 us)
Async XLA Ops:
  0.6 31.1 %copy-start = (f32[1,1,256,256]{3,2,1,0:T(8,128)S(1)}, f32[1,1,256,256]{3,2,1,0:T(8,128)}, u32[]{:S(2)}) copy-start(f32[1,1,256,256]{3,2,1,0:T(8,128)} %param.15) | copy-start | bytes 786436
  0.6 20.5 %copy-start.1 = (f32[64,256]{1,0:T(8,128)S(1)}, f32[64,256]{1,0:T(8,128)}, u32[]{:S(2)}) copy-start(f32[64,256]{1,0:T(8,128)} %param.12) | copy-start | bytes 196612
  0.7 22.6 %copy-start.2 = (f32[64,256]{1,0:T(8,128)S(1)}, f32[64,256]{1,0:T(8,128)}, u32[]{:S(2)}) copy-start(f32[64,256]{1,0:T(8,128)} %param.11) | copy-start | bytes 196612
  0.7 39.3 %copy-start.4 = (s32[1,1,256]{2,1,0:T(1,128)S(1)}, s32[1,1,256]{2,1,0:T(1,128)}, u32[]{:S(2)}) copy-start(s32[1,1,256]{2,1,0:T(1,128)} %param.14) | copy-start | bytes 3076
  0.7 25.9 %copy-start.3 = (f32[64,256]{1,0:T(8,128)S(1)}, f32[64,256]{1,0:T(8,128)}, u32[]{:S(2)}) copy-start(f32[64,256]{1,0:T(8,128)} %param.10) | copy-start | bytes 196612
  1.8 19.5 %collective-permute-start = (f32[4,1,256]{2,1,0:T(1,128)S(1)}, f32[4,1,256]{2,1,0:T(1,128)S(1)}, u32[]{:S(2)}, u32[]{:S(2)}) collective-permute-start(f32[4,1,256]{2,1,0:T(1,128)S(1)} %get-tuple-element.26), channel_id=1, source_target_pairs={{4,0},{8,4},{12,8},{16,12},{20,16},{24,20},{28,24},{0,28},{5,1},{9... | collective-permute-start | bytes 12296 | tf_op jit(solution)/shard_map/ppermute | solution.py:16
  7.8 13.4 %collective-permute-start.2 = (f32[4,1,256]{2,1,0:T(1,128)S(1)}, f32[4,1,256]{2,1,0:T(1,128)S(1)}, u32[]{:S(2)}, u32[]{:S(2)}) collective-permute-start(f32[4,1,256]{2,1,0:T(1,128)S(1)} %get-tuple-element.25), channel_id=1, source_target_pairs={{0,4},{4,8},{8,12},{12,16},{16,20},{20,24},{24,28},{28,0},{1,5},{5... | collective-permute-start | bytes 12296 | tf_op jit(solution)/shard_map/ppermute | solution.py:14
  8.6 12.5 %collective-permute-start.4 = (f32[64,1]{1,0:T(8,128)S(1)}, f32[64,1]{1,0:T(8,128)S(1)}, u32[]{:S(2)}, u32[]{:S(2)}) collective-permute-start(f32[64,1]{1,0:T(8,128)S(1)} %slice.138), channel_id=1, source_target_pairs={{0,1},{1,2},{2,3},{3,0},{4,5},{5,6},{6,7},{7,4},{8,9},{9,10},{10,1... | collective-permute-start | bytes 776 | tf_op jit(solution)/shard_map/ppermute | solution.py:26
  9.4 13.9 %collective-permute-start.1 = (f32[1,256]{1,0:T(1,128)S(1)}, f32[1,256]{1,0:T(1,128)S(1)}, u32[]{:S(2)}, u32[]{:S(2)}) collective-permute-start(f32[1,256]{1,0:T(1,128)S(1)} %slice.132), channel_id=1, source_target_pairs={{0,4},{4,8},{8,12},{12,16},{16,20},{20,24},{24,28},{28,0},{1,5},{5... | collective-permute-start | bytes 3080 | tf_op jit(solution)/shard_map/ppermute | solution.py:26
  21.4 4.6 %collective-permute-start.5 = (f32[4,66,1]{2,1,0:T(8,128)S(1)}, f32[4,66,1]{2,1,0:T(8,128)S(1)}, u32[]{:S(2)}, u32[]{:S(2)}) collective-permute-start(f32[4,66,1]{2,1,0:T(8,128)S(1)} %get-tuple-element.18), channel_id=1, source_target_pairs={{0,1},{1,2},{2,3},{3,0},{4,5},{5,6},{6,7},{7,4},{8,9},{9,10},{10,1... | collective-permute-start | bytes 3176 | tf_op jit(solution)/shard_map/ppermute | solution.py:14
  23.1 3.6 %collective-permute-start.3 = (f32[4,66,1]{2,1,0:T(8,128)S(1)}, f32[4,66,1]{2,1,0:T(8,128)S(1)}, u32[]{:S(2)}, u32[]{:S(2)}) collective-permute-start(f32[4,66,1]{2,1,0:T(8,128)S(1)} %get-tuple-element.17), channel_id=1, source_target_pairs={{1,0},{2,1},{3,2},{0,3},{5,4},{6,5},{7,6},{4,7},{9,8},{10,9},{11,1... | collective-permute-start | bytes 3176 | tf_op jit(solution)/shard_map/ppermute | solution.py:16
  26.9 6.1 %collective-permute-start.6 = (f32[4,1,256]{2,1,0:T(1,128)S(1)}, f32[4,1,256]{2,1,0:T(1,128)S(1)}, u32[]{:S(2)}, u32[]{:S(2)}) collective-permute-start(f32[4,1,256]{2,1,0:T(1,128)S(1)} %get-tuple-element.24), channel_id=1, source_target_pairs={{4,0},{8,4},{12,8},{16,12},{20,16},{24,20},{28,24},{0,28},{5,1},{9... | collective-permute-start | bytes 12296 | tf_op jit(solution)/shard_map/ppermute | solution.py:16
  31.7 6.3 %collective-permute-start.7 = (f32[4,1,256]{2,1,0:T(1,128)S(1)}, f32[4,1,256]{2,1,0:T(1,128)S(1)}, u32[]{:S(2)}, u32[]{:S(2)}) collective-permute-start(f32[4,1,256]{2,1,0:T(1,128)S(1)} %get-tuple-element.23), channel_id=1, source_target_pairs={{0,4},{4,8},{8,12},{12,16},{16,20},{20,24},{24,28},{28,0},{1,5},{5... | collective-permute-start | bytes 12296 | tf_op jit(solution)/shard_map/ppermute | solution.py:14
  38.1 12.3 %collective-permute-start.9 = (f32[4,66,1]{2,1,0:T(8,128)S(1)}, f32[4,66,1]{2,1,0:T(8,128)S(1)}, u32[]{:S(2)}, u32[]{:S(2)}) collective-permute-start(f32[4,66,1]{2,1,0:T(8,128)S(1)} %get-tuple-element.16), channel_id=1, source_target_pairs={{0,1},{1,2},{2,3},{3,0},{4,5},{5,6},{6,7},{7,4},{8,9},{9,10},{10,1... | collective-permute-start | bytes 3176 | tf_op jit(solution)/shard_map/ppermute | solution.py:14
  38.2 12.3 %collective-permute-start.8 = (f32[4,66,1]{2,1,0:T(8,128)S(1)}, f32[4,66,1]{2,1,0:T(8,128)S(1)}, u32[]{:S(2)}, u32[]{:S(2)}) collective-permute-start(f32[4,66,1]{2,1,0:T(8,128)S(1)} %get-tuple-element.15), channel_id=1, source_target_pairs={{1,0},{2,1},{3,2},{0,3},{5,4},{6,5},{7,6},{4,7},{9,8},{10,9},{11,1... | collective-permute-start | bytes 3176 | tf_op jit(solution)/shard_map/ppermute | solution.py:16
  88.2 5.4 %collective-permute-start.10 = (f32[4,1,256]{2,1,0:T(1,128)S(1)}, f32[4,1,256]{2,1,0:T(1,128)S(1)}, u32[]{:S(2)}, u32[]{:S(2)}) collective-permute-start(f32[4,1,256]{2,1,0:T(1,128)S(1)} %get-tuple-element.22), channel_id=1, source_target_pairs={{4,0},{8,4},{12,8},{16,12},{20,16},{24,20},{28,24},{0,28},{5,1},{9... | collective-permute-start | bytes 12296 | tf_op jit(solution)/shard_map/ppermute | solution.py:16
  92.2 6.3 %collective-permute-start.11 = (f32[4,1,256]{2,1,0:T(1,128)S(1)}, f32[4,1,256]{2,1,0:T(1,128)S(1)}, u32[]{:S(2)}, u32[]{:S(2)}) collective-permute-start(f32[4,1,256]{2,1,0:T(1,128)S(1)} %get-tuple-element.21), channel_id=1, source_target_pairs={{0,4},{4,8},{8,12},{12,16},{16,20},{20,24},{24,28},{28,0},{1,5},{5... | collective-permute-start | bytes 12296 | tf_op jit(solution)/shard_map/ppermute | solution.py:14
  98.7 4.6 %collective-permute-start.13 = (f32[4,66,1]{2,1,0:T(8,128)S(1)}, f32[4,66,1]{2,1,0:T(8,128)S(1)}, u32[]{:S(2)}, u32[]{:S(2)}) collective-permute-start(f32[4,66,1]{2,1,0:T(8,128)S(1)} %get-tuple-element.14), channel_id=1, source_target_pairs={{0,1},{1,2},{2,3},{3,0},{4,5},{5,6},{6,7},{7,4},{8,9},{9,10},{10,1... | collective-permute-start | bytes 3176 | tf_op jit(solution)/shard_map/ppermute | solution.py:14
  98.7 5.2 %collective-permute-start.12 = (f32[4,66,1]{2,1,0:T(8,128)S(1)}, f32[4,66,1]{2,1,0:T(8,128)S(1)}, u32[]{:S(2)}, u32[]{:S(2)}) collective-permute-start(f32[4,66,1]{2,1,0:T(8,128)S(1)} %get-tuple-element.13), channel_id=1, source_target_pairs={{1,0},{2,1},{3,2},{0,3},{5,4},{6,5},{7,6},{4,7},{9,8},{10,9},{11,1... | collective-permute-start | bytes 3176 | tf_op jit(solution)/shard_map/ppermute | solution.py:16
  104.3 10.9 %collective-permute-start.14 = (f32[4,1,256]{2,1,0:T(1,128)S(1)}, f32[4,1,256]{2,1,0:T(1,128)S(1)}, u32[]{:S(2)}, u32[]{:S(2)}) collective-permute-start(f32[4,1,256]{2,1,0:T(1,128)S(1)} %get-tuple-element.20), channel_id=1, source_target_pairs={{4,0},{8,4},{12,8},{16,12},{20,16},{24,20},{28,24},{0,28},{5,1},{9... | collective-permute-start | bytes 12296 | tf_op jit(solution)/shard_map/ppermute | solution.py:16
  104.3 10.8 %collective-permute-start.15 = (f32[4,1,256]{2,1,0:T(1,128)S(1)}, f32[4,1,256]{2,1,0:T(1,128)S(1)}, u32[]{:S(2)}, u32[]{:S(2)}) collective-permute-start(f32[4,1,256]{2,1,0:T(1,128)S(1)} %get-tuple-element.19), channel_id=1, source_target_pairs={{0,4},{4,8},{8,12},{12,16},{16,20},{20,24},{24,28},{28,0},{1,5},{5... | collective-permute-start | bytes 12296 | tf_op jit(solution)/shard_map/ppermute | solution.py:14
  115.3 12.6 %collective-permute-start.17 = (f32[4,66,1]{2,1,0:T(8,128)S(1)}, f32[4,66,1]{2,1,0:T(8,128)S(1)}, u32[]{:S(2)}, u32[]{:S(2)}) collective-permute-start(f32[4,66,1]{2,1,0:T(8,128)S(1)} %get-tuple-element.12), channel_id=1, source_target_pairs={{0,1},{1,2},{2,3},{3,0},{4,5},{5,6},{6,7},{7,4},{8,9},{9,10},{10,1... | collective-permute-start | bytes 3176 | tf_op jit(solution)/shard_map/ppermute | solution.py:14
  115.8 12.1 %collective-permute-start.16 = (f32[4,66,1]{2,1,0:T(8,128)S(1)}, f32[4,66,1]{2,1,0:T(8,128)S(1)}, u32[]{:S(2)}, u32[]{:S(2)}) collective-permute-start(f32[4,66,1]{2,1,0:T(8,128)S(1)} %get-tuple-element.11), channel_id=1, source_target_pairs={{1,0},{2,1},{3,2},{0,3},{5,4},{6,5},{7,6},{4,7},{9,8},{10,9},{11,1... | collective-permute-start | bytes 3176 | tf_op jit(solution)/shard_map/ppermute | solution.py:16
where the time goes:
time: 212 us; the launch traced here: 211 us
  blocking collectives  116 us (55%)
  local copies, waits for them, and re-layouts  31 us (15%)
  starting transfers between devices  24.2 us (11%)
  waiting for transfers between devices  19.3 us (9%)
  other arithmetic  16.5 us (8%)
  between operations  3.4 us (2%)
    psum x1, blocking collectives, per_device(): total = lax.psum(jnp.sum(probes * solution), ('gx', 'gy'))  41.2 us
    psum x1, blocking collectives, per_device(): lax.psum((jnp.sum(residual * residual, axis=(1, 2)), jnp.sum(residual * r...  38.3 us
    psum x1, blocking collectives, curvature(): return lax.psum(jnp.sum(first * second, axis=(1, 2)), ('gx', 'gy'))  36.9 us
    ppermute x8, starting transfers between devices, with_halo(): lax.ppermute(head, axis, [((i + 1) % count, i) for i in range(count)])  19.9 us
    ppermute x8, waiting for transfers between devices, with_halo(): lax.ppermute(tail, axis, [(i, (i + 1) % count) for i in range(count)])  15.5 us
    reshape x2, local copies, waits for them, and re-layouts, observe(): jnp.zeros_like(flat).at[:, cell_ids].add(weighted).reshape(field.shape)  10.5 us
    scatter-add x2, other arithmetic, observe(): jnp.zeros_like(flat).at[:, cell_ids].add(weighted).reshape(field.shape)  10.3 us
    gather x4, local copies, waits for them, and re-layouts, observe(): sampled = jnp.take(flat, cell_ids, axis=1) * mask  8.35 us
  transfers between devices with their start and end apart: 18, of which 8 were waited for; matrix products, arithmetic and copies ran while one was open for 20% of the time, Pallas kernels for 0%

commit v1 on v0

--- a/solution.py
+++ b/solution.py
@@ -2,6 +2,11 @@
 import jax.numpy as jnp
 from jax import lax
 from jax.sharding import PartitionSpec as P
+
+
+def axis_by_axis(array, inner_axis, outer_axis):
+    half = lax.psum(array, inner_axis)
+    return lax.psum(half, outer_axis)
 
 
 def with_halo(cells, sides, width):
@@ -98,12 +103,13 @@
     solution = first_step[:, None, None] * probes
     residual = probes - first_step[:, None, None] * image
     residual_image = hessian(residual)
-    norm_next, product = lax.psum(
+    norm_next, product = axis_by_axis(
         (
             jnp.sum(residual * residual, axis=(1, 2)),
             jnp.sum(residual * residual_image, axis=(1, 2)),
         ),
-        ("gx", "gy"),
+        "gx",
+        "gy",
     )
     ratio = norm_next / norm_start
     direction = residual + ratio[:, None, None] * probes

time: 212 us -> 196 us (0.925)
  blocking collectives: 116 us -> 99.4 us
    psum x1 -> x2, blocking collectives: 38.3 us -> 25.5 us  [the longest x1 19.9 us: axis_by_axis(): half = lax.psum(array, inner_axis)]
    psum x1, blocking collectives: 41.2 us -> 37 us  [per_device(): total = lax.psum(jnp.sum(probes * solution), ('gx', 'gy'))]
  transfers between devices with their start and end apart: 18 -> 18, of which waited for: 8 -> 8; matrix products, arithmetic and copies ran while one was open for 20% -> 22% of each run, Pallas kernels for 0% -> 0%
where the time goes in v1:
time: 196 us; the launch traced here: 194 us
  blocking collectives  99.4 us (51%)
  local copies, waits for them, and re-layouts  31 us (16%)
  starting transfers between devices  24.2 us (12%)
  waiting for transfers between devices  19.3 us (10%)
  other arithmetic  16.5 us (8%)
  between operations  3.4 us (2%)
    psum x1, blocking collectives, per_device(): total = lax.psum(jnp.sum(probes * solution), ('gx', 'gy'))  37 us
    psum x1, blocking collectives, curvature(): return lax.psum(jnp.sum(first * second, axis=(1, 2)), ('gx', 'gy'))  36.9 us
    ppermute x8, starting transfers between devices, with_halo(): lax.ppermute(head, axis, [((i + 1) % count, i) for i in range(count)])  19.9 us
    psum x1, blocking collectives, axis_by_axis(): half = lax.psum(array, inner_axis)  19.9 us
    ppermute x8, waiting for transfers between devices, with_halo(): lax.ppermute(tail, axis, [(i, (i + 1) % count) for i in range(count)])  15.5 us
    reshape x2, local copies, waits for them, and re-layouts, observe(): jnp.zeros_like(flat).at[:, cell_ids].add(weighted).reshape(field.shape)  10.5 us
    scatter-add x2, other arithmetic, observe(): jnp.zeros_like(flat).at[:, cell_ids].add(weighted).reshape(field.shape)  10.3 us
    gather x4, local copies, waits for them, and re-layouts, observe(): sampled = jnp.take(flat, cell_ids, axis=1) * mask  8.35 us
  transfers between devices with their start and end apart: 18, of which 8 were waited for; matrix products, arithmetic and copies ran while one was open for 22% of the time, Pallas kernels for 0%

profile of v1, /device:TPU:0, one launch (start us, length us, event | category | flops | bytes accessed | tf_op | source)
XLA Modules:
  0.0 194.2 jit_solution(14259969784255963918)
XLA Ops:
  0.6 0.0 copy-start
  0.6 0.0 copy-start.1
  0.7 0.0 copy-start.2
  0.7 0.0 copy-start.4
  0.7 0.7 broadcast_multiply_fusion.1
  1.5 0.1 broadcast_add_fusion
  1.5 0.2 add_convert_fusion.1
  1.8 6.1 %collective-permute-start = (f32[4,1,256]{2,1,0:T(1,128)S(1)}, f32[4,1,256]{2,1,0:T(1,128)S(1)}, u32[]{:S(2)}, u32[]{:S(2)}) collective-permute-start(f32[4,1,256]{2,1,0:T(1,128)S(1)} %get-tuple-element.28), channel_id=1, source_target_pairs={{4,0},{8,4},{12,8},{16,12},{20,16},{24,20},{28,24},{0,28},{5,1},{9... | collective-permute-start | bytes 12296 | tf_op jit(solution)/shard_map/ppermute | solution.py:21
  7.8 0.0 collective-permute-start.2
  7.8 0.8 slice.138
  8.6 0.7 slice.132
  9.4 0.2 copy.33
  9.6 0.7 compare_select_fusion.1
  10.9 0.7 compare_and_fusion
  11.6 0.2 add_convert_fusion
  11.9 5.1 %copy.25 = f32[4,16384]{0,1:T(8,128)} copy(f32[4,16384]{1,0:T(4,128)S(1)} %add_convert_fusion) | data formatting | bytes 524288 | tf_op jit(solution)/shard_map/convert_element_type | solution.py:44
  16.9 4.1 %gather_fusion = f32[256,4]{1,0:T(8,128)S(1)} fusion(f32[4,16384]{0,1:T(8,128)} %copy.25, s32[1024]{0:T(1024)S(1)} %pad_clamp_fusion), kind=kCustom, calls=%fused_computation.clone | custom fusion | bytes 9216 | tf_op jit(solution)/shard_map/jit(_take)/gather | solution.py:87
  21.0 0.1 copy.26
  21.1 0.1 pad_maximum_fusion.36
  21.3 0.1 fusion.80
  21.4 1.7 collective-permute-start.5
  23.1 0.2 collective-permute-start.3
  23.3 2.7 %collective-permute-done.5 = f32[4,66,1]{2,1,0:T(8,128)S(1)} collective-permute-done((f32[4,66,1]{2,1,0:T(8,128)S(1)}, f32[4,66,1]{2,1,0:T(8,128)S(1)}, u32[]{:S(2)}, u32[]{:S(2)}) %collective-permute-start.5) | collective-permute-done | bytes 1088 | tf_op jit(solution)/shard_map/ppermute | solution.py:19
  26.0 0.6 collective-permute-done.3
  26.6 0.3 fusion.54
  26.9 4.8 %collective-permute-start.6 = (f32[4,1,256]{2,1,0:T(1,128)S(1)}, f32[4,1,256]{2,1,0:T(1,128)S(1)}, u32[]{:S(2)}, u32[]{:S(2)}) collective-permute-start(f32[4,1,256]{2,1,0:T(1,128)S(1)} %get-tuple-element.26), channel_id=1, source_target_pairs={{4,0},{8,4},{12,8},{16,12},{20,16},{24,20},{28,24},{0,28},{5,1},{9... | collective-permute-start | bytes 12296 | tf_op jit(solution)/shard_map/ppermute | solution.py:21
  31.7 0.2 fusion.5
  31.9 1.1 collective-permute-done.6
  33.0 5.0 %collective-permute-done.7 = f32[4,1,256]{2,1,0:T(1,128)S(1)} collective-permute-done((f32[4,1,256]{2,1,0:T(1,128)S(1)}, f32[4,1,256]{2,1,0:T(1,128)S(1)}, u32[]{:S(2)}, u32[]{:S(2)}) %collective-permute-start.7) | collective-permute-done | bytes 4128 | tf_op jit(solution)/shard_map/ppermute | solution.py:19
  38.0 0.1 fusion.79
  38.1 0.1 collective-permute-start.9
  38.2 1.7 collective-permute-start.8
  40.0 0.1 copy.27
  40.1 5.1 %scatter_custom_fusion = f32[4,16384]{0,1:T(8,128)} fusion(s32[256]{0:T(256)S(1)} %bitcast.37, f32[256,4]{1,0:T(8,128)S(1)} %copy.27, f32[]{:T(128)} %constant.53.clone.1), kind=kCustom, calls=%fused_computation.6 | custom fusion | flops 1024 | bytes 262148 | tf_op jit(solution)/shard_map/scatter-add | solution.py:90
  45.2 5.2 %copy.28 = f32[4,64,256]{2,1,0:T(8,128)S(1)} copy(f32[4,64,256]{0,2,1:T(8,128)} %bitcast.31) | data formatting | bytes 524288 | tf_op jit(solution)/shard_map/reshape | solution.py:90
  50.5 0.5 multiply_reduce_fusion.2
  51.0 36.9 %psum.42 = f32[4]{0:T(128)S(1)} all-reduce(f32[4]{0:T(128)S(1)} %get-tuple-element.11), channel_id=1, replica_groups=mesh['gx'=8,'gy'=4] {'gx','gy'}, use_global_device_ids=true, to_apply=%region_2.4 | all-reduce | flops 4 | bytes 32 | tf_op jit(solution)/shard_map/psum | solution.py:63
  87.9 0.3 multiply_reduce_fusion.1
  88.2 4.0 %collective-permute-start.10 = (f32[4,1,256]{2,1,0:T(1,128)S(1)}, f32[4,1,256]{2,1,0:T(1,128)S(1)}, u32[]{:S(2)}, u32[]{:S(2)}) collective-permute-start(f32[4,1,256]{2,1,0:T(1,128)S(1)} %get-tuple-element.24), channel_id=1, source_target_pairs={{4,0},{8,4},{12,8},{16,12},{20,16},{24,20},{28,24},{0,28},{5,1},{9... | collective-permute-start | bytes 12296 | tf_op jit(solution)/shard_map/ppermute | solution.py:21
  92.3 1.3 collective-permute-done.10
  93.6 5.0 %collective-permute-done.11 = f32[4,1,256]{2,1,0:T(1,128)S(1)} collective-permute-done((f32[4,1,256]{2,1,0:T(1,128)S(1)}, f32[4,1,256]{2,1,0:T(1,128)S(1)}, u32[]{:S(2)}, u32[]{:S(2)}) %collective-permute-start.11) | collective-permute-done | bytes 4128 | tf_op jit(solution)/shard_map/ppermute | solution.py:19
  98.6 0.1 fusion.78
  98.7 0.1 collective-permute-start.13
  98.8 1.7 collective-permute-start.12
  100.5 2.8 %collective-permute-done.13 = f32[4,66,1]{2,1,0:T(8,128)S(1)} collective-permute-done((f32[4,66,1]{2,1,0:T(8,128)S(1)}, f32[4,66,1]{2,1,0:T(8,128)S(1)}, u32[]{:S(2)}, u32[]{:S(2)}) %collective-permute-start.13) | collective-permute-done | bytes 1088 | tf_op jit(solution)/shard_map/ppermute | solution.py:19
  103.3 0.7 collective-permute-done.12
  104.0 0.3 fusion.29
  104.3 0.1 collective-permute-start.14
  104.4 2.0 %collective-permute-start.15 = (f32[4,1,256]{2,1,0:T(1,128)S(1)}, f32[4,1,256]{2,1,0:T(1,128)S(1)}, u32[]{:S(2)}, u32[]{:S(2)}) collective-permute-start(f32[4,1,256]{2,1,0:T(1,128)S(1)} %get-tuple-element.21), channel_id=1, source_target_pairs={{0,4},{4,8},{8,12},{12,16},{16,20},{20,24},{24,28},{28,0},{1,5},{5... | collective-permute-start | bytes 12296 | tf_op jit(solution)/shard_map/ppermute | solution.py:19
  106.4 4.6 %copy.29 = f32[4,64,256]{0,2,1:T(8,128)} copy(f32[4,64,256]{2,1,0:T(8,128)S(1)} %get-tuple-element.10) | data formatting | bytes 524288 | tf_op jit(solution)/shard_map/sub | solution.py:104
  111.0 4.1 %gather_fusion.1 = f32[256,4]{1,0:T(8,128)S(1)} fusion(f32[4,16384]{0,1:T(8,128)} %bitcast.32, s32[1024]{0:T(1024)S(1)} %pad_clamp_fusion), kind=kCustom, calls=%fused_computation.1.clone | custom fusion | bytes 9216 | tf_op jit(solution)/shard_map/jit(_take)/gather | solution.py:87
  115.1 0.1 copy.30
  115.2 0.1 fusion.77
  115.3 0.5 collective-permute-start.17
  115.8 1.3 collective-permute-start.16
  117.1 0.2 fusion.4
  117.3 0.2 copy.31
  117.5 5.1 %scatter_custom_fusion.1 = f32[4,16384]{0,1:T(8,128)} fusion(s32[256]{0:T(256)S(1)} %bitcast.38, f32[256,4]{1,0:T(8,128)S(1)} %copy.31, f32[]{:T(128)} %constant.53.clone.1), kind=kCustom, calls=%fused_computation.4 | custom fusion | flops 1024 | bytes 262148 | tf_op jit(solution)/shard_map/scatter-add | solution.py:90
  122.7 5.2 %copy.32 = f32[4,64,256]{2,1,0:T(8,128)S(1)} copy(f32[4,64,256]{0,2,1:T(8,128)} %bitcast.30) | data formatting | bytes 524288 | tf_op jit(solution)/shard_map/reshape | solution.py:90
  127.9 0.4 fusion.17
  128.3 19.9 %all-reduce = (f32[4]{0:T(128)S(1)}, f32[4]{0:T(128)S(1)}) all-reduce(f32[4]{0:T(128)S(1)} %get-tuple-element.9, f32[4]{0:T(128)S(1)} %fusion.17), channel_id=1, replica_groups=mesh['gx'=8,'gy'=4] {'gx'}, use_global_device_ids=true, to_apply=%region_4.6 | all-reduce | flops 8 | bytes 64 | tf_op jit(solution)/shard_map/psum | solution.py:8
  148.2 5.6 %all-reduce.1 = (f32[4]{0:T(128)S(1)}, f32[4]{0:T(128)S(1)}) all-reduce(f32[4]{0:T(128)S(1)} %get-tuple-element.3, f32[4]{0:T(128)S(1)} %get-tuple-element.4), channel_id=1, replica_groups=mesh['gx'=8,'gy'=4] {'gy'}, use_global_device_ids=true, to_apply=%region_5.7 | all-reduce | flops 8 | bytes 64 | tf_op jit(solution)/shard_map/psum | solution.py:9
  153.8 1.6 multiply_reduce_fusion
  155.4 37.0 %psum.47 = f32[]{:T(128)} all-reduce(f32[]{:T(128)} %get-tuple-element.7), channel_id=1, replica_groups=mesh['gx'=8,'gy'=4] {'gx','gy'}, use_global_device_ids=true, to_apply=%region_11.13 | all-reduce | flops 1 | bytes 8 | tf_op jit(solution)/shard_map/psum | solution.py:118
  (37 shorter events, 0.3 us)
Async XLA Ops:
  0.6 31.1 %copy-start = (f32[1,1,256,256]{3,2,1,0:T(8,128)S(1)}, f32[1,1,256,256]{3,2,1,0:T(8,128)}, u32[]{:S(2)}) copy-start(f32[1,1,256,256]{3,2,1,0:T(8,128)} %param.15) | copy-start | bytes 786436
  0.6 20.5 %copy-start.1 = (f32[64,256]{1,0:T(8,128)S(1)}, f32[64,256]{1,0:T(8,128)}, u32[]{:S(2)}) copy-start(f32[64,256]{1,0:T(8,128)} %param.12) | copy-start | bytes 196612
  0.7 22.6 %copy-start.2 = (f32[64,256]{1,0:T(8,128)S(1)}, f32[64,256]{1,0:T(8,128)}, u32[]{:S(2)}) copy-start(f32[64,256]{1,0:T(8,128)} %param.11) | copy-start | bytes 196612
  0.7 39.3 %copy-start.4 = (s32[1,1,256]{2,1,0:T(1,128)S(1)}, s32[1,1,256]{2,1,0:T(1,128)}, u32[]{:S(2)}) copy-start(s32[1,1,256]{2,1,0:T(1,128)} %param.14) | copy-start | bytes 3076
  0.7 25.9 %copy-start.3 = (f32[64,256]{1,0:T(8,128)S(1)}, f32[64,256]{1,0:T(8,128)}, u32[]{:S(2)}) copy-start(f32[64,256]{1,0:T(8,128)} %param.10) | copy-start | bytes 196612
  1.8 19.5 %collective-permute-start = (f32[4,1,256]{2,1,0:T(1,128)S(1)}, f32[4,1,256]{2,1,0:T(1,128)S(1)}, u32[]{:S(2)}, u32[]{:S(2)}) collective-permute-start(f32[4,1,256]{2,1,0:T(1,128)S(1)} %get-tuple-element.28), channel_id=1, source_target_pairs={{4,0},{8,4},{12,8},{16,12},{20,16},{24,20},{28,24},{0,28},{5,1},{9... | collective-permute-start | bytes 12296 | tf_op jit(solution)/shard_map/ppermute | solution.py:21
  7.8 13.4 %collective-permute-start.2 = (f32[4,1,256]{2,1,0:T(1,128)S(1)}, f32[4,1,256]{2,1,0:T(1,128)S(1)}, u32[]{:S(2)}, u32[]{:S(2)}) collective-permute-start(f32[4,1,256]{2,1,0:T(1,128)S(1)} %get-tuple-element.27), channel_id=1, source_target_pairs={{0,4},{4,8},{8,12},{12,16},{16,20},{20,24},{24,28},{28,0},{1,5},{5... | collective-permute-start | bytes 12296 | tf_op jit(solution)/shard_map/ppermute | solution.py:19
  8.6 12.5 %collective-permute-start.4 = (f32[64,1]{1,0:T(8,128)S(1)}, f32[64,1]{1,0:T(8,128)S(1)}, u32[]{:S(2)}, u32[]{:S(2)}) collective-permute-start(f32[64,1]{1,0:T(8,128)S(1)} %slice.138), channel_id=1, source_target_pairs={{0,1},{1,2},{2,3},{3,0},{4,5},{5,6},{6,7},{7,4},{8,9},{9,10},{10,1... | collective-permute-start | bytes 776 | tf_op jit(solution)/shard_map/ppermute | solution.py:31
  9.4 13.9 %collective-permute-start.1 = (f32[1,256]{1,0:T(1,128)S(1)}, f32[1,256]{1,0:T(1,128)S(1)}, u32[]{:S(2)}, u32[]{:S(2)}) collective-permute-start(f32[1,256]{1,0:T(1,128)S(1)} %slice.132), channel_id=1, source_target_pairs={{0,4},{4,8},{8,12},{12,16},{16,20},{20,24},{24,28},{28,0},{1,5},{5... | collective-permute-start | bytes 3080 | tf_op jit(solution)/shard_map/ppermute | solution.py:31
  21.4 4.6 %collective-permute-start.5 = (f32[4,66,1]{2,1,0:T(8,128)S(1)}, f32[4,66,1]{2,1,0:T(8,128)S(1)}, u32[]{:S(2)}, u32[]{:S(2)}) collective-permute-start(f32[4,66,1]{2,1,0:T(8,128)S(1)} %get-tuple-element.20), channel_id=1, source_target_pairs={{0,1},{1,2},{2,3},{3,0},{4,5},{5,6},{6,7},{7,4},{8,9},{9,10},{10,1... | collective-permute-start | bytes 3176 | tf_op jit(solution)/shard_map/ppermute | solution.py:19
  23.1 3.6 %collective-permute-start.3 = (f32[4,66,1]{2,1,0:T(8,128)S(1)}, f32[4,66,1]{2,1,0:T(8,128)S(1)}, u32[]{:S(2)}, u32[]{:S(2)}) collective-permute-start(f32[4,66,1]{2,1,0:T(8,128)S(1)} %get-tuple-element.19), channel_id=1, source_target_pairs={{1,0},{2,1},{3,2},{0,3},{5,4},{6,5},{7,6},{4,7},{9,8},{10,9},{11,1... | collective-permute-start | bytes 3176 | tf_op jit(solution)/shard_map/ppermute | solution.py:21
  26.9 6.1 %collective-permute-start.6 = (f32[4,1,256]{2,1,0:T(1,128)S(1)}, f32[4,1,256]{2,1,0:T(1,128)S(1)}, u32[]{:S(2)}, u32[]{:S(2)}) collective-permute-start(f32[4,1,256]{2,1,0:T(1,128)S(1)} %get-tuple-element.26), channel_id=1, source_target_pairs={{4,0},{8,4},{12,8},{16,12},{20,16},{24,20},{28,24},{0,28},{5,1},{9... | collective-permute-start | bytes 12296 | tf_op jit(solution)/shard_map/ppermute | solution.py:21
  31.7 6.3 %collective-permute-start.7 = (f32[4,1,256]{2,1,0:T(1,128)S(1)}, f32[4,1,256]{2,1,0:T(1,128)S(1)}, u32[]{:S(2)}, u32[]{:S(2)}) collective-permute-start(f32[4,1,256]{2,1,0:T(1,128)S(1)} %get-tuple-element.25), channel_id=1, source_target_pairs={{0,4},{4,8},{8,12},{12,16},{16,20},{20,24},{24,28},{28,0},{1,5},{5... | collective-permute-start | bytes 12296 | tf_op jit(solution)/shard_map/ppermute | solution.py:19
  38.1 12.3 %collective-permute-start.9 = (f32[4,66,1]{2,1,0:T(8,128)S(1)}, f32[4,66,1]{2,1,0:T(8,128)S(1)}, u32[]{:S(2)}, u32[]{:S(2)}) collective-permute-start(f32[4,66,1]{2,1,0:T(8,128)S(1)} %get-tuple-element.18), channel_id=1, source_target_pairs={{0,1},{1,2},{2,3},{3,0},{4,5},{5,6},{6,7},{7,4},{8,9},{9,10},{10,1... | collective-permute-start | bytes 3176 | tf_op jit(solution)/shard_map/ppermute | solution.py:19
  38.2 12.3 %collective-permute-start.8 = (f32[4,66,1]{2,1,0:T(8,128)S(1)}, f32[4,66,1]{2,1,0:T(8,128)S(1)}, u32[]{:S(2)}, u32[]{:S(2)}) collective-permute-start(f32[4,66,1]{2,1,0:T(8,128)S(1)} %get-tuple-element.17), channel_id=1, source_target_pairs={{1,0},{2,1},{3,2},{0,3},{5,4},{6,5},{7,6},{4,7},{9,8},{10,9},{11,1... | collective-permute-start | bytes 3176 | tf_op jit(solution)/shard_map/ppermute | solution.py:21
  88.2 5.4 %collective-permute-start.10 = (f32[4,1,256]{2,1,0:T(1,128)S(1)}, f32[4,1,256]{2,1,0:T(1,128)S(1)}, u32[]{:S(2)}, u32[]{:S(2)}) collective-permute-start(f32[4,1,256]{2,1,0:T(1,128)S(1)} %get-tuple-element.24), channel_id=1, source_target_pairs={{4,0},{8,4},{12,8},{16,12},{20,16},{24,20},{28,24},{0,28},{5,1},{9... | collective-permute-start | bytes 12296 | tf_op jit(solution)/shard_map/ppermute | solution.py:21
  92.3 6.3 %collective-permute-start.11 = (f32[4,1,256]{2,1,0:T(1,128)S(1)}, f32[4,1,256]{2,1,0:T(1,128)S(1)}, u32[]{:S(2)}, u32[]{:S(2)}) collective-permute-start(f32[4,1,256]{2,1,0:T(1,128)S(1)} %get-tuple-element.23), channel_id=1, source_target_pairs={{0,4},{4,8},{8,12},{12,16},{16,20},{20,24},{24,28},{28,0},{1,5},{5... | collective-permute-start | bytes 12296 | tf_op jit(solution)/shard_map/ppermute | solution.py:19
  98.7 4.6 %collective-permute-start.13 = (f32[4,66,1]{2,1,0:T(8,128)S(1)}, f32[4,66,1]{2,1,0:T(8,128)S(1)}, u32[]{:S(2)}, u32[]{:S(2)}) collective-permute-start(f32[4,66,1]{2,1,0:T(8,128)S(1)} %get-tuple-element.16), channel_id=1, source_target_pairs={{0,1},{1,2},{2,3},{3,0},{4,5},{5,6},{6,7},{7,4},{8,9},{9,10},{10,1... | collective-permute-start | bytes 3176 | tf_op jit(solution)/shard_map/ppermute | solution.py:19
  98.8 5.2 %collective-permute-start.12 = (f32[4,66,1]{2,1,0:T(8,128)S(1)}, f32[4,66,1]{2,1,0:T(8,128)S(1)}, u32[]{:S(2)}, u32[]{:S(2)}) collective-permute-start(f32[4,66,1]{2,1,0:T(8,128)S(1)} %get-tuple-element.15), channel_id=1, source_target_pairs={{1,0},{2,1},{3,2},{0,3},{5,4},{6,5},{7,6},{4,7},{9,8},{10,9},{11,1... | collective-permute-start | bytes 3176 | tf_op jit(solution)/shard_map/ppermute | solution.py:21
  104.3 10.9 %collective-permute-start.14 = (f32[4,1,256]{2,1,0:T(1,128)S(1)}, f32[4,1,256]{2,1,0:T(1,128)S(1)}, u32[]{:S(2)}, u32[]{:S(2)}) collective-permute-start(f32[4,1,256]{2,1,0:T(1,128)S(1)} %get-tuple-element.22), channel_id=1, source_target_pairs={{4,0},{8,4},{12,8},{16,12},{20,16},{24,20},{28,24},{0,28},{5,1},{9... | collective-permute-start | bytes 12296 | tf_op jit(solution)/shard_map/ppermute | solution.py:21
  104.4 10.8 %collective-permute-start.15 = (f32[4,1,256]{2,1,0:T(1,128)S(1)}, f32[4,1,256]{2,1,0:T(1,128)S(1)}, u32[]{:S(2)}, u32[]{:S(2)}) collective-permute-start(f32[4,1,256]{2,1,0:T(1,128)S(1)} %get-tuple-element.21), channel_id=1, source_target_pairs={{0,4},{4,8},{8,12},{12,16},{16,20},{20,24},{24,28},{28,0},{1,5},{5... | collective-permute-start | bytes 12296 | tf_op jit(solution)/shard_map/ppermute | solution.py:19
  115.3 12.6 %collective-permute-start.17 = (f32[4,66,1]{2,1,0:T(8,128)S(1)}, f32[4,66,1]{2,1,0:T(8,128)S(1)}, u32[]{:S(2)}, u32[]{:S(2)}) collective-permute-start(f32[4,66,1]{2,1,0:T(8,128)S(1)} %get-tuple-element.14), channel_id=1, source_target_pairs={{0,1},{1,2},{2,3},{3,0},{4,5},{5,6},{6,7},{7,4},{8,9},{9,10},{10,1... | collective-permute-start | bytes 3176 | tf_op jit(solution)/shard_map/ppermute | solution.py:19
  115.8 12.1 %collective-permute-start.16 = (f32[4,66,1]{2,1,0:T(8,128)S(1)}, f32[4,66,1]{2,1,0:T(8,128)S(1)}, u32[]{:S(2)}, u32[]{:S(2)}) collective-permute-start(f32[4,66,1]{2,1,0:T(8,128)S(1)} %get-tuple-element.13), channel_id=1, source_target_pairs={{1,0},{2,1},{3,2},{0,3},{5,4},{6,5},{7,6},{4,7},{9,8},{10,9},{11,1... | collective-permute-start | bytes 3176 | tf_op jit(solution)/shard_map/ppermute | solution.py:21
